TPU v7x, 8 devices: a whole 2x2x1 slice. The times are simulated.
8 devices in a mesh: dp: 1 (over z), tp: 8 (over y, x, core).
Axes of the slice: x: 2, y: 2, z: 1, core: 2. Of those that a mesh axis runs over, the one named last changes fastest.
Arguments:
- enc_out: bfloat16 [128, 192, 512], P('dp')
- w_proj: bfloat16 [512, 1024], P(None, 'tp')
- labels: int32 [128, 48], P('dp')
- in_len: int32 [128], P('dp')
- lab_len: int32 [128], P('dp')
Outputs:
- output 1: float32 [128], P('dp')
- output 2: float32 [512, 1024], P('dp', 'tp')
- output 3: float32 [128, 192, 512], P('dp')
All inputs are finite; a program needn't handle non-finite values.
Results may differ from a plain program's by a relative error of at most 0.001.
Values are sent between devices in bfloat16 or wider.
A program may use at most 1 GiB of HBM per device.

v0:
```python
import functools

import jax
import jax.numpy as jnp
from jax import lax
from jax.experimental import pallas as pl
from jax.experimental.pallas import tpu as pltpu
from jax.sharding import PartitionSpec as P

NEG_FILL = -1.0e30
CH = 32
NCH = 8
PITCH = 104
DUMMY = 55
UNR = 4
MESH = pl.DeviceIdType.MESH
F32 = jnp.float32
BF16 = jnp.bfloat16


def gather_kernel(n, w_ref, out_ref, send_sem, recv_sem):
    me = lax.axis_index("tp")
    barrier = pltpu.get_barrier_semaphore()
    for i in range(1, n):
        peer = lax.rem(me + i, n)
        pl.semaphore_signal(barrier, inc=1, device_id={"tp": peer}, device_id_type=MESH)
    pl.semaphore_wait(barrier, n - 1)
    copies = []
    for i in range(1, n):
        peer = lax.rem(me + i, n)
        copy = pltpu.make_async_remote_copy(
            src_ref=w_ref,
            dst_ref=out_ref.at[me],
            send_sem=send_sem.at[i],
            recv_sem=recv_sem.at[i],
            device_id={"tp": peer},
            device_id_type=MESH,
        )
        copy.start()
        copies.append(copy)
    out_ref[me] = w_ref[...]
    for copy in copies:
        copy.wait()


def take_lanes(x, idx):
    return jnp.take_along_axis(x, idx, axis=1, mode="promise_in_bounds")


def lse2(a, b):
    top = jnp.maximum(a, b)
    return top + jnp.log(1.0 + jnp.exp(jnp.minimum(a, b) - top))


def ctc_kernel(
    n_seq, n_frames, n_lab,
    in_len, labt_ref, inrow_ref, lenrow_ref, enc_hbm, wg_hbm,
    loss_ref, gw_ref, ghs_hbm,
    enc_v, w_v, wt_v, oh_v, gl_v, eo_v, et_v, ab_v, inv_v, nxt_v, z0_v, z1_v, g0_v, g1_v, h0_v, h1_v, top_v, sum_v, lse_v, gwt_v, lacc_v, zero_v, flag_v,
    tabb, tabt, flag_s, enc_sem, w_sem, gh_sem, zero_sem, flag_sem,
):
    me = lax.axis_index("tp")
    n_vocab = w_v.shape[1]
    n_blk = n_vocab // 128
    n_grp = n_seq // 4
    mid = n_frames // 2
    n_per = n_frames // CH
    per_mid = mid // CH

    def enc_copy(g):
        rows = pl.ds(pl.multiple_of(4 * g * n_frames, 4 * n_frames), 4 * n_frames)
        return pltpu.make_async_copy(enc_hbm.at[rows], enc_v.at[rows], enc_sem.at[g])

    w_copies = [pltpu.make_async_copy(wg_hbm.at[k], w_v.at[:, pl.ds(k * 128, 128)], w_sem.at[k]) for k in range(n_blk)]
    for copy in w_copies:
        copy.start()

    @pl.loop(0, n_grp)
    def _(g):
        enc_copy(g).start()

    for ref in (zero_v, lacc_v, gwt_v, z0_v, z1_v, g0_v, g1_v):
        ref[...] = jnp.zeros_like(ref)
    for j in range(4 * NCH):
        tabb[j] = 0
        tabt[j] = 0

    def zero_copy(b, j):
        return pltpu.make_async_copy(zero_v, ghs_hbm.at[pl.ds(pl.multiple_of(b * n_frames + j * CH, CH), CH)], zero_sem)

    sub48 = lax.broadcasted_iota(jnp.int32, (48, 128), 0)
    in_row = inrow_ref[...]
    len_row = lenrow_ref[...]
    lab48 = jnp.where(sub48 < len_row, labt_ref[...], -1 - sub48)
    skip = lab48 != pltpu.roll(lab48, 1, 0)

    nxt = jnp.full((48, 128), DUMMY, jnp.int32)
    later = jnp.zeros((48, 128), jnp.int32)
    for d in range(n_lab - 1, 0, -1):
        same = (pltpu.roll(lab48, 48 - d, 0) == lab48) & (sub48 < 48 - d)
        nxt = jnp.where(same, sub48 + d, nxt)
        later = later + jnp.where(same, 1, 0)
    nxt_f = jnp.concatenate([nxt.astype(F32), jnp.full((16, 128), float(DUMMY), F32)], axis=0)
    nxt_v[...] = jnp.concatenate([nxt_f, nxt_f + 64.0], axis=0).T.astype(jnp.int32)
    flag_v[...] = jnp.broadcast_to(jnp.max(later.astype(F32), axis=0, keepdims=True), (8, 128)).astype(jnp.int32)
    flag_copy = pltpu.make_async_copy(flag_v, flag_s, flag_sem)
    flag_copy.start()

    for copy in w_copies:
        copy.wait()
    wt_v[...] = w_v[...].T
    row16 = lax.broadcasted_iota(jnp.int32, (16, wt_v.shape[1]), 0)
    tail = jnp.where(row16 == 0, wt_v[0:16, :].astype(F32), 0.0).astype(BF16)
    for k in range(8):
        gl_v[k * 64 + 48:(k + 1) * 64, :] = tail

    lane48 = lax.broadcasted_iota(jnp.int32, (48, 128), 1)
    sub48f = sub48.astype(F32)
    lane1 = lax.broadcasted_iota(jnp.int32, (1, 128), 1)
    lane_mid = lax.broadcasted_iota(jnp.int32, (mid, 128), 1)

    def emit_group(g, n):
        for k in range(4):
            b = 4 * g + k
            cnt = (in_len[b] + CH - 1) // CH
            for j in range(n_per):
                tabb[4 * NCH + n + j] = b
                tabt[4 * NCH + n + j] = j * CH

                @pl.when(j >= cnt)
                def _():
                    zero_copy(b, j).start()
            n = n + cnt
            col = take_lanes(lab48, jnp.full((48, 128), b, jnp.int32))
            firsts = []
            for j in range(n_blk):
                hit = col == lane48 + 128 * j
                oh_v[k * 48:(k + 1) * 48, j * 128:(j + 1) * 128] = jnp.where(hit, 1.0, 0.0).astype(BF16)
                start = jnp.where(lane1 == 0, 48.0, float(DUMMY)) if j == 0 else float(DUMMY)
                firsts.append(jnp.minimum(jnp.min(jnp.where(hit, sub48f, float(DUMMY)), axis=0, keepdims=True), start))
            inv_v[pl.ds(pl.multiple_of(b * 8, 8), 8), :] = jnp.concatenate(firsts, axis=0).astype(jnp.int32)
        picked = jnp.dot(oh_v[...], wt_v[...], preferred_element_type=F32).astype(BF16)
        enc_copy(g).wait()
        for k in range(4):
            for h in range(2):
                gl_v[k * 128 + h * 64:k * 128 + h * 64 + 48, :] = picked[k * 48:(k + 1) * 48]
        for k in range(4):
            b = 4 * g + k
            x = enc_v[pl.ds(pl.multiple_of(b * n_frames, n_frames), n_frames), :]
            e = lax.dot_general(x, gl_v[k * 128:(k + 1) * 128, :], (((1,), (1,)), ((), ())), preferred_element_type=F32)
            eo_v[pl.ds(pl.multiple_of(b * PITCH, 8), mid), :] = jnp.where(lane_mid < 64, e[0:mid], e[mid:n_frames])
        return n

    n_live = lax.fori_loop(0, n_grp, emit_group, 0)
    for j in range(4 * NCH):
        tabb[4 * NCH + n_live + j] = 0
        tabt[4 * NCH + n_live + j] = 0
    n_iter = (n_live + NCH - 1) // NCH

    def turn_emissions(jj, acc):
        for u in range(UNR):
            j = jj * UNR + u
            turned = eo_v[pl.ds(j, n_seq, stride=PITCH), :].T
            low = turned[48:49]
            high = turned[112:113]
            et_v[pl.ds(pl.multiple_of(j * 48, 8), 48), :] = turned[0:48] - low
            et_v[pl.ds(pl.multiple_of((j + mid) * 48, 8), 48), :] = turned[64:112] - high
            acc = acc + jnp.where(j < in_row, low, 0.0) + jnp.where(j + mid < in_row, high, 0.0)
        return acc

    blank_sum = lax.fori_loop(0, mid // UNR, turn_emissions, jnp.zeros((1, 128), F32))

    neg8 = jnp.full((8, 128), NEG_FILL, F32)
    sub56 = lax.broadcasted_iota(jnp.int32, (56, 128), 0)
    skip56 = jnp.concatenate([jnp.where(skip, 1.0, 0.0), jnp.zeros((8, 128), F32)], axis=0) > 0.5

    def emit_at(t):
        return et_v[pl.ds(pl.multiple_of(t * 48, 8), 48), :]

    def alpha_step(t, blk, lab):
        shifted = pltpu.roll(jnp.concatenate([lab, neg8], axis=0), 1, 0)
        blk_new = lse2(blk, shifted)
        via = jnp.where(skip, blk_new[0:48], blk[0:48])
        lab_new = lse2(lab, via) + emit_at(t)
        live = t < in_row
        return jnp.where(live, blk_new, blk), jnp.where(live, lab_new, lab)

    def beta_step(t, blk, lab):
        emitted = lab + emit_at(t + 1)
        blk_new = lse2(blk, jnp.concatenate([emitted, neg8], axis=0))
        via = jnp.where(skip56, blk_new, blk)
        lab_new = lse2(emitted, pltpu.roll(via, 55, 0)[0:48])
        live = t + 1 < in_row
        return jnp.where(live, blk_new, blk), jnp.where(live, lab_new, lab)

    def keep(t, blk, lab):
        row = pl.multiple_of(t * 104, 8)
        ab_v[pl.ds(row, 56), :] = blk
        ab_v[pl.ds(row + 56, 48), :] = lab

    a_blk = jnp.where(sub56 == 0, 0.0, NEG_FILL).astype(F32) + jnp.zeros((56, 128), F32)
    a_lab = jnp.full((48, 128), NEG_FILL, F32)
    b_blk = jnp.where(sub56 == len_row, 0.0, NEG_FILL).astype(F32)
    b_lab = jnp.where(sub48 == len_row - 1, 0.0, NEG_FILL).astype(F32)

    a_blk, a_lab = alpha_step(0, a_blk, a_lab)
    keep(0, a_blk, a_lab)
    keep(n_frames - 1, b_blk, b_lab)

    def first_half(k, state):
        a_blk, a_lab, b_blk, b_lab = state
        a_blk, a_lab = alpha_step(k, a_blk, a_lab)
        keep(k, a_blk, a_lab)
        t = n_frames - 1 - k
        b_blk, b_lab = beta_step(t, b_blk, b_lab)
        keep(t, b_blk, b_lab)
        return a_blk, a_lab, b_blk, b_lab

    a_blk, a_lab, b_blk, b_lab = lax.fori_loop(1, mid, first_half, (a_blk, a_lab, b_blk, b_lab))

    m_blk, m_lab = beta_step(mid - 1, b_blk, b_lab)
    s_blk = a_blk + m_blk
    s_lab = a_lab + m_lab
    top = jnp.maximum(jnp.max(s_blk, axis=0, keepdims=True), jnp.max(s_lab, axis=0, keepdims=True))
    total = jnp.sum(jnp.exp(s_blk - top), axis=0, keepdims=True) + jnp.sum(jnp.exp(s_lab - top), axis=0, keepdims=True)
    log_z = top + jnp.log(total)
    sub8 = lax.broadcasted_iota(jnp.int32, (8, 128), 0)

    def put_occ(t, blk, lab):
        row = pl.multiple_of(t * 104, 8)
        occ_blk = jnp.sum(jnp.exp(ab_v[pl.ds(row, 56), :] + (blk - log_z)), axis=0, keepdims=True)
        occ_lab = jnp.exp(ab_v[pl.ds(row + 56, 48), :] + (lab - log_z))
        ab_v[pl.ds(row, 48), :] = occ_lab
        ab_v[pl.ds(row + 48, 8), :] = jnp.where(sub8 == 0, occ_blk, 0.0)

    def second_half(k, state):
        a_blk, a_lab, b_blk, b_lab = state
        a_blk, a_lab = alpha_step(k, a_blk, a_lab)
        t = n_frames - 1 - k
        b_blk, b_lab = beta_step(t, b_blk, b_lab)
        put_occ(k, a_blk, a_lab)
        put_occ(t, b_blk, b_lab)
        return a_blk, a_lab, b_blk, b_lab

    lax.fori_loop(mid, n_frames, second_half, (a_blk, a_lab, b_blk, b_lab))

    zero8 = jnp.zeros((8, 128), F32)

    @pl.loop(0, mid // UNR)
    def _(jj):
        for u in range(UNR):
            j = jj * UNR + u
            low = ab_v[pl.ds(pl.multiple_of(j * 104, 8), 56), :]
            high = ab_v[pl.ds(pl.multiple_of((j + mid) * 104, 8), 56), :]
            turned = jnp.concatenate([low, zero8, high, zero8], axis=0).T
            eo_v[pl.ds(j, n_seq, stride=PITCH), :] = turned + take_lanes(turned, nxt_v[...])

    flag_copy.wait()

    @pl.loop(0, n_seq)
    def _(b):
        @pl.when(flag_s[0, b] > 1)
        def _():
            rows = pl.ds(pl.multiple_of(b * PITCH, 8), mid)
            count = flag_s[0, b]
            rounds = sum((count >= 2 ** r).astype(jnp.int32) for r in range(1, 6))

            def more(_, link):
                link = take_lanes(link, link)
                occ = eo_v[rows, :]
                eo_v[rows, :] = occ + take_lanes(occ, jnp.broadcast_to(link[0:1], (mid, 128)))
                return link

            lax.fori_loop(0, rounds, more, jnp.broadcast_to(nxt_v[pl.ds(b, 1), :], (8, 128)))

    row_ids = lax.broadcasted_iota(jnp.int32, (CH, 128), 0)
    own = pl.ds(pl.multiple_of(me * 128, 128), 128)

    def chunk(i, c):
        idx = i * NCH + c
        return tabb[idx + 4 * NCH], tabt[idx + 4 * NCH], (idx >= 0) & (idx < n_live)

    def enc_rows(i):
        parts = []
        for c in range(NCH):
            b, t0, _ = chunk(i, c)
            parts.append(enc_v[pl.ds(pl.multiple_of(b * n_frames + t0, CH), CH), :])
        return jnp.concatenate(parts, axis=0)

    def gh_copy(i, c, h_v, par):
        b, t0, _ = chunk(i, c)
        row = pl.multiple_of(b * n_frames + t0, CH)
        return pltpu.make_async_copy(h_v.at[pl.ds(c * CH, CH)], ghs_hbm.at[pl.ds(row, CH)], gh_sem.at[par, c])

    def gh_wait(i, h_v, par):
        for c in range(NCH):
            @pl.when(chunk(i, c)[2])
            def _():
                gh_copy(i, c, h_v, par).wait()

    def stage(i, zw, zr, gwr, gr, h_v, par):
        gh_wait(i - 4, h_v, par)
        zw[...] = jnp.dot(enc_rows(i), w_v[...], preferred_element_type=F32)
        for r in range(NCH * CH // 8):
            rows = slice(r * 8, (r + 1) * 8)
            z = zr[rows, :]
            parts = [z[:, j * 128:(j + 1) * 128] for j in range(n_blk)]
            top = functools.reduce(jnp.maximum, parts)
            top_v[rows, :] = top
            sum_v[rows, :] = functools.reduce(jnp.add, [jnp.exp(part - top) for part in parts])
        tops = top_v[...]
        top = jnp.max(tops, axis=1, keepdims=True)
        lse_v[...] = jnp.broadcast_to(top + jnp.log(jnp.sum(sum_v[...] * jnp.exp(tops - top), axis=1, keepdims=True)), (NCH * CH, 128))
        for c in range(NCH):
            b, t0, ok = chunk(i - 1, c)
            rows = slice(c * CH, (c + 1) * CH)
            live = row_ids < jnp.where(ok, in_len[b], 0) - t0
            lse = lse_v[rows, :]
            lacc_v[pl.ds(b, 1), :] += jnp.sum(jnp.where(live, lse, 0.0), axis=0, keepdims=True)
            lse = jnp.where(live, lse, 3.0e38)
            upper = (t0 >= mid).astype(jnp.int32)
            occ = jnp.where(live, eo_v[pl.ds(pl.multiple_of(b * PITCH + t0 - upper * mid, 8), CH), :], 0.0)
            inv = inv_v[pl.ds(pl.multiple_of(b * 8, 8), 8), :] + upper * 64
            for j in range(n_blk):
                cols = slice(j * 128, (j + 1) * 128)
                col_occ = take_lanes(occ, jnp.broadcast_to(inv[j:j + 1], (CH, 128)))
                gwr[rows, cols] = (jnp.exp(zr[rows, cols] - lse) - col_occ).astype(BF16)
        h_v[...] = jnp.dot(gr[...], wt_v[...], preferred_element_type=F32)
        gwt_v[...] += lax.dot_general(gr[:, own], enc_rows(i - 2), (((0,), (0,)), ((), ())), preferred_element_type=F32)
        for c in range(NCH):
            @pl.when(chunk(i - 2, c)[2])
            def _():
                gh_copy(i - 2, c, h_v, par).start()

    trips = (n_iter + 3) // 2

    @pl.loop(0, trips)
    def _(ii):
        stage(2 * ii, z0_v, z1_v, g1_v, g0_v, h0_v, 0)
        stage(2 * ii + 1, z1_v, z0_v, g0_v, g1_v, h1_v, 1)

    gh_wait(2 * trips - 4, h0_v, 0)
    gh_wait(2 * trips - 3, h1_v, 1)
    gw_ref[...] = gwt_v[...].T
    loss_ref[...] = lacc_v[...].T[0:1, :] - blank_sum - log_z

    @pl.loop(0, n_seq)
    def _(b):
        cnt = (in_len[b] + CH - 1) // CH
        for j in range(n_per):
            @pl.when(j >= cnt)
            def _():
                zero_copy(b, j).wait()


def solution(mesh):
    n_dev = mesh.shape["tp"]

    def device_fn(enc_out, w_loc, labels, in_len, lab_len):
        n_seq, n_frames, hidden = enc_out.shape
        n_lab = labels.shape[1]
        n_cols = w_loc.shape[1]
        n_vocab = n_cols * n_dev
        vmem = pl.BlockSpec(memory_space=pltpu.VMEM)
        smem = pl.BlockSpec(memory_space=pltpu.SMEM)
        anyspace = pl.BlockSpec(memory_space=pl.ANY)
        w_all = pl.pallas_call(
            functools.partial(gather_kernel, n_dev),
            out_shape=jax.ShapeDtypeStruct((n_dev, hidden, n_cols), BF16),
            in_specs=[vmem],
            out_specs=vmem,
            scratch_shapes=[pltpu.SemaphoreType.DMA((n_dev,)), pltpu.SemaphoreType.DMA((n_dev,))],
            compiler_params=pltpu.CompilerParams(collective_id=0, has_side_effects=True),
            name="gather_w",
        )(w_loc)
        n_per = n_frames // CH
        n_grp = n_seq // 4
        loss, grad_w, grad_hs = pl.pallas_call(
            functools.partial(ctc_kernel, n_seq, n_frames, n_lab),
            out_shape=(
                jax.ShapeDtypeStruct((1, n_seq), F32),
                jax.ShapeDtypeStruct((hidden, n_cols), F32),
                jax.ShapeDtypeStruct((n_seq * n_frames, hidden), F32),
            ),
            in_specs=[smem, vmem, vmem, vmem, anyspace, anyspace],
            out_specs=(vmem, vmem, anyspace),
            scratch_shapes=[
                pltpu.VMEM((n_seq * n_frames, hidden), BF16),
                pltpu.VMEM((hidden, n_vocab), BF16),
                pltpu.VMEM((n_vocab, hidden), BF16),
                pltpu.VMEM((192, n_vocab), BF16),
                pltpu.VMEM((512, hidden), BF16),
                pltpu.VMEM((n_seq * PITCH, 128), F32),
                pltpu.VMEM((n_frames * 48, 128), F32),
                pltpu.VMEM((n_frames * 104, 128), F32),
                pltpu.VMEM((n_seq * n_dev, 128), jnp.int32),
                pltpu.VMEM((n_seq, 128), jnp.int32),
                pltpu.VMEM((NCH * CH, n_vocab), F32),
                pltpu.VMEM((NCH * CH, n_vocab), F32),
                pltpu.VMEM((NCH * CH, n_vocab), BF16),
                pltpu.VMEM((NCH * CH, n_vocab), BF16),
                pltpu.VMEM((NCH * CH, hidden), F32),
                pltpu.VMEM((NCH * CH, hidden), F32),
                pltpu.VMEM((NCH * CH, 128), F32),
                pltpu.VMEM((NCH * CH, 128), F32),
                pltpu.VMEM((NCH * CH, 128), F32),
                pltpu.VMEM((n_cols, hidden), F32),
                pltpu.VMEM((n_seq, 128), F32),
                pltpu.VMEM((CH, hidden), F32),
                pltpu.VMEM((8, 128), jnp.int32),
                pltpu.SMEM((n_seq * n_per + 10 * NCH,), jnp.int32),
                pltpu.SMEM((n_seq * n_per + 10 * NCH,), jnp.int32),
                pltpu.SMEM((8, 128), jnp.int32),
                pltpu.SemaphoreType.DMA((n_grp,)),
                pltpu.SemaphoreType.DMA((n_dev,)),
                pltpu.SemaphoreType.DMA((2, NCH)),
                pltpu.SemaphoreType.DMA,
                pltpu.SemaphoreType.DMA,
            ],
            compiler_params=pltpu.CompilerParams(vmem_limit_bytes=63 * 1024 * 1024),
            name="ctc",
        )(in_len, labels.T, in_len.reshape(1, n_seq), lab_len.reshape(1, n_seq), enc_out.reshape(n_seq * n_frames, hidden), w_all)
        return loss.reshape(n_seq), grad_w, grad_hs.reshape(n_seq, n_frames, hidden)

    return jax.shard_map(device_fn, mesh=mesh, in_specs=(P("dp"), P(None, "tp"), P("dp"), P("dp"), P("dp")), out_specs=(P("dp"), P("dp", "tp"), P("dp")), check_vma=False)
```

profile of v0, /device:TPU:1, one launch (start us, length us, event | category | flops | bytes accessed | tf_op | source)
XLA Modules:
  0.0 150.1 jit_solution(11639560421197323263)
XLA Ops:
  0.6 18.1 %gather_w.1.wg_hbm = bf16[8,512,128]{2,1,0:T(8,128)(2,1)} custom-call(bf16[512,128]{1,0:T(8,128)(2,1)} %w_ref.1), custom_call_target="tpu_custom_call" | custom-call | tf_op jit(solution)/shard_map/gather_w/pallas_call | solution.py:367
  18.7 131.4 %ctc.1 = (f32[1,128]{1,0:T(1,128)}, f32[512,128]{1,0:T(8,128)}, f32[24576,512]{1,0:T(8,128)}) custom-call(s32[128]{0:T(128)} %in_len.1, s32[48,128]{1,0:T(8,128)} %bitcast.7, s32[1,128]{1,0:T(1,128)} %bitcast.8, s32[1,128]{1,0:T(1,128)} %bitcast.9, bf16[24576,512]{1,0:T(8,128)(2,1)} %bitcast.6, bf16[8,512,128]{2,1,0:T(8,128)(2,1)} %gather_w.1.wg_hbm), custom_call_target="tpu_custom_call" | custom-call | tf_op jit(solution)/shard_map/ctc/pallas_call | solution.py:378
where the time goes:
time: 151 us; the launch traced here: 150 us
  Pallas kernels  149 us (99%)
    pallas_call x1, Pallas kernels, device_fn(): pl.pallas_call(functools.partial(ctc_kernel, n_seq, n_frames, n_lab), out...  131 us
    pallas_call x1, Pallas kernels, device_fn(): pl.pallas_call(functools.partial(gather_kernel, n_dev), out_shape=jax.Sha...  18.1 us

commit v1 on v0

--- a/solution.py
+++ b/solution.py
@@ -10,37 +10,55 @@
 NEG_FILL = -1.0e30
 CH = 32
 NCH = 8
+PAD = 8 * NCH
 PITCH = 104
 DUMMY = 55
 UNR = 4
+AHEAD = 6
 MESH = pl.DeviceIdType.MESH
 F32 = jnp.float32
 BF16 = jnp.bfloat16
 
 
-def gather_kernel(n, w_ref, out_ref, send_sem, recv_sem):
+def gather_kernel(w_ref, out_ref, send_sem, recv_sem):
     me = lax.axis_index("tp")
+    core, col, row = lax.rem(me, 2), lax.rem(me // 2, 2), me // 4
+    mate = me + 1 - 2 * core
+    across = me + 2 * (1 - 2 * col)
+    along = me + 4 * (1 - 2 * row)
+    far = across + along - me
     barrier = pltpu.get_barrier_semaphore()
-    for i in range(1, n):
-        peer = lax.rem(me + i, n)
+    for peer in (mate, across, along):
         pl.semaphore_signal(barrier, inc=1, device_id={"tp": peer}, device_id_type=MESH)
-    pl.semaphore_wait(barrier, n - 1)
-    copies = []
-    for i in range(1, n):
-        peer = lax.rem(me + i, n)
+    pl.semaphore_wait(barrier, 3)
+    rows = w_ref.shape[0]
+    upper, lower = pl.ds(0, rows // 2), pl.ds(rows // 2, rows // 2)
+
+    def push(k, src, dst, peer):
         copy = pltpu.make_async_remote_copy(
-            src_ref=w_ref,
-            dst_ref=out_ref.at[me],
-            send_sem=send_sem.at[i],
-            recv_sem=recv_sem.at[i],
-            device_id={"tp": peer},
-            device_id_type=MESH,
+            src_ref=src, dst_ref=dst, send_sem=send_sem.at[k], recv_sem=recv_sem.at[k],
+            device_id={"tp": peer}, device_id_type=MESH,
         )
         copy.start()
-        copies.append(copy)
+        return copy
+
+    own = out_ref.at[me]
+    copies = [push(1, w_ref, own, across), push(2, w_ref, own, along), push(0, w_ref, own, mate)]
     out_ref[me] = w_ref[...]
+    copies[0].wait_recv()
+    copies.append(push(4, out_ref.at[across, upper], out_ref.at[across, upper], along))
+    copies.append(push(3, out_ref.at[across], out_ref.at[across], mate))
+    copies[1].wait_recv()
+    copies.append(push(6, out_ref.at[along, lower], out_ref.at[along, lower], across))
+    copies.append(push(5, out_ref.at[along], out_ref.at[along], mate))
+    copies[3].wait_recv()
+    copies.append(push(7, out_ref.at[far, upper], out_ref.at[far, upper], mate))
+    copies[5].wait_recv()
+    copies.append(push(8, out_ref.at[far, lower], out_ref.at[far, lower], mate))
+    for k in (2, 4, 6, 7, 8):
+        copies[k].wait_recv()
     for copy in copies:
-        copy.wait()
+        copy.wait_send()
 
 
 def take_lanes(x, idx):
@@ -56,7 +74,7 @@
     n_seq, n_frames, n_lab,
     in_len, labt_ref, inrow_ref, lenrow_ref, enc_hbm, wg_hbm,
     loss_ref, gw_ref, ghs_hbm,
-    enc_v, w_v, wt_v, oh_v, gl_v, eo_v, et_v, ab_v, inv_v, nxt_v, z0_v, z1_v, g0_v, g1_v, h0_v, h1_v, top_v, sum_v, lse_v, gwt_v, lacc_v, zero_v, flag_v,
+    enc_v, w_v, wt_v, oh0_v, oh1_v, gl0_v, gl1_v, eo_v, et_v, ab_v, inv_v, nxt_v, z0_v, z1_v, g0_v, g1_v, h0_v, h1_v, top_v, sum_v, lse_v, gwt_v, lacc_v, zero_v, flag_v,
     tabb, tabt, flag_s, enc_sem, w_sem, gh_sem, zero_sem, flag_sem,
 ):
     me = lax.axis_index("tp")
@@ -75,13 +93,12 @@
     for copy in w_copies:
         copy.start()
 
-    @pl.loop(0, n_grp)
-    def _(g):
+    for g in range(AHEAD):
         enc_copy(g).start()
 
     for ref in (zero_v, lacc_v, gwt_v, z0_v, z1_v, g0_v, g1_v):
         ref[...] = jnp.zeros_like(ref)
-    for j in range(4 * NCH):
+    for j in range(PAD):
         tabb[j] = 0
         tabt[j] = 0
 
@@ -112,25 +129,31 @@
     row16 = lax.broadcasted_iota(jnp.int32, (16, wt_v.shape[1]), 0)
     tail = jnp.where(row16 == 0, wt_v[0:16, :].astype(F32), 0.0).astype(BF16)
     for k in range(8):
-        gl_v[k * 64 + 48:(k + 1) * 64, :] = tail
+        gl0_v[k * 64 + 48:(k + 1) * 64, :] = tail
+        gl1_v[k * 64 + 48:(k + 1) * 64, :] = tail
 
     lane48 = lax.broadcasted_iota(jnp.int32, (48, 128), 1)
     sub48f = sub48.astype(F32)
     lane1 = lax.broadcasted_iota(jnp.int32, (1, 128), 1)
     lane_mid = lax.broadcasted_iota(jnp.int32, (mid, 128), 1)
 
-    def emit_group(g, n):
+    def list_group(g, n):
         for k in range(4):
-            b = 4 * g + k
-            cnt = (in_len[b] + CH - 1) // CH
+            b = jnp.minimum(4 * g + k, n_seq - 1)
+            cnt = jnp.where(g < n_grp, (in_len[b] + CH - 1) // CH, n_per)
             for j in range(n_per):
-                tabb[4 * NCH + n + j] = b
-                tabt[4 * NCH + n + j] = j * CH
+                tabb[PAD + n + j] = b
+                tabt[PAD + n + j] = j * CH
 
                 @pl.when(j >= cnt)
                 def _():
                     zero_copy(b, j).start()
-            n = n + cnt
+            n = n + jnp.where(g < n_grp, cnt, 0)
+        return n
+
+    def build_hot(g, oh_v):
+        for k in range(4):
+            b = 4 * g + k
             col = take_lanes(lab48, jnp.full((48, 128), b, jnp.int32))
             firsts = []
             for j in range(n_blk):
@@ -139,22 +162,45 @@
                 start = jnp.where(lane1 == 0, 48.0, float(DUMMY)) if j == 0 else float(DUMMY)
                 firsts.append(jnp.minimum(jnp.min(jnp.where(hit, sub48f, float(DUMMY)), axis=0, keepdims=True), start))
             inv_v[pl.ds(pl.multiple_of(b * 8, 8), 8), :] = jnp.concatenate(firsts, axis=0).astype(jnp.int32)
+
+    def pick_cols(oh_v, gl_v):
         picked = jnp.dot(oh_v[...], wt_v[...], preferred_element_type=F32).astype(BF16)
-        enc_copy(g).wait()
         for k in range(4):
             for h in range(2):
                 gl_v[k * 128 + h * 64:k * 128 + h * 64 + 48, :] = picked[k * 48:(k + 1) * 48]
+
+    def emit_group(g, gl_v):
         for k in range(4):
             b = 4 * g + k
             x = enc_v[pl.ds(pl.multiple_of(b * n_frames, n_frames), n_frames), :]
             e = lax.dot_general(x, gl_v[k * 128:(k + 1) * 128, :], (((1,), (1,)), ((), ())), preferred_element_type=F32)
             eo_v[pl.ds(pl.multiple_of(b * PITCH, 8), mid), :] = jnp.where(lane_mid < 64, e[0:mid], e[mid:n_frames])
+
+    build_hot(0, oh0_v)
+
+    def emit_pair(ii, n):
+        for s in range(2):
+            g = 2 * ii + s
+
+            @pl.when((g >= 1) & (g <= n_grp))
+            def _():
+                enc_copy(g - 1).wait()
+
+            @pl.when(g + AHEAD < n_grp)
+            def _():
+                enc_copy(g + AHEAD).start()
+        n = list_group(2 * ii + 1, list_group(2 * ii, n))
+        for s in range(2):
+            g = 2 * ii + s
+            build_hot(jnp.minimum(g + 1, n_grp - 1), (oh1_v, oh0_v)[s])
+            pick_cols((oh0_v, oh1_v)[s], (gl0_v, gl1_v)[s])
+            emit_group(jnp.clip(g - 1, 0, n_grp - 1), (gl1_v, gl0_v)[s])
         return n
 
-    n_live = lax.fori_loop(0, n_grp, emit_group, 0)
-    for j in range(4 * NCH):
-        tabb[4 * NCH + n_live + j] = 0
-        tabt[4 * NCH + n_live + j] = 0
+    n_live = lax.fori_loop(0, n_grp // 2 + 1, emit_pair, 0)
+    for j in range(PAD):
+        tabb[PAD + n_live + j] = 0
+        tabt[PAD + n_live + j] = 0
     n_iter = (n_live + NCH - 1) // NCH
 
     def turn_emissions(jj, acc):
@@ -235,14 +281,17 @@
 
     def second_half(k, state):
         a_blk, a_lab, b_blk, b_lab = state
+        t = n_frames - 1 - k
+        put_occ(k - 1, a_blk, a_lab)
+        put_occ(t + 1, b_blk, b_lab)
         a_blk, a_lab = alpha_step(k, a_blk, a_lab)
-        t = n_frames - 1 - k
         b_blk, b_lab = beta_step(t, b_blk, b_lab)
-        put_occ(k, a_blk, a_lab)
-        put_occ(t, b_blk, b_lab)
         return a_blk, a_lab, b_blk, b_lab
 
-    lax.fori_loop(mid, n_frames, second_half, (a_blk, a_lab, b_blk, b_lab))
+    a_blk, a_lab = alpha_step(mid, a_blk, a_lab)
+    a_blk, a_lab, b_blk, b_lab = lax.fori_loop(mid + 1, n_frames, second_half, (a_blk, a_lab, m_blk, m_lab))
+    put_occ(n_frames - 1, a_blk, a_lab)
+    put_occ(0, b_blk, b_lab)
 
     zero8 = jnp.zeros((8, 128), F32)
 
@@ -257,8 +306,7 @@
 
     flag_copy.wait()
 
-    @pl.loop(0, n_seq)
-    def _(b):
+    def more_rounds(b):
         @pl.when(flag_s[0, b] > 1)
         def _():
             rows = pl.ds(pl.multiple_of(b * PITCH, 8), mid)
@@ -273,12 +321,22 @@
 
             lax.fori_loop(0, rounds, more, jnp.broadcast_to(nxt_v[pl.ds(b, 1), :], (8, 128)))
 
+    @pl.loop(0, n_seq // 16)
+    def _(bb):
+        most = functools.reduce(jnp.maximum, [flag_s[0, bb * 16 + u] for u in range(16)])
+
+        @pl.when(most > 1)
+        def _():
+            @pl.loop(0, 16)
+            def _(u):
+                more_rounds(bb * 16 + u)
+
     row_ids = lax.broadcasted_iota(jnp.int32, (CH, 128), 0)
     own = pl.ds(pl.multiple_of(me * 128, 128), 128)
 
     def chunk(i, c):
         idx = i * NCH + c
-        return tabb[idx + 4 * NCH], tabt[idx + 4 * NCH], (idx >= 0) & (idx < n_live)
+        return tabb[idx + PAD], tabt[idx + PAD], (idx >= 0) & (idx < n_live)
 
     def enc_rows(i):
         parts = []
@@ -298,8 +356,13 @@
             def _():
                 gh_copy(i, c, h_v, par).wait()
 
-    def stage(i, zw, zr, gwr, gr, h_v, par):
-        gh_wait(i - 4, h_v, par)
+    def gh_start(i, h_v, par):
+        for c in range(NCH):
+            @pl.when(chunk(i, c)[2])
+            def _():
+                gh_copy(i, c, h_v, par).start()
+
+    def stage(i, zw, zr, gwr, gr, h_v):
         zw[...] = jnp.dot(enc_rows(i), w_v[...], preferred_element_type=F32)
         for r in range(NCH * CH // 8):
             rows = slice(r * 8, (r + 1) * 8)
@@ -327,30 +390,30 @@
                 gwr[rows, cols] = (jnp.exp(zr[rows, cols] - lse) - col_occ).astype(BF16)
         h_v[...] = jnp.dot(gr[...], wt_v[...], preferred_element_type=F32)
         gwt_v[...] += lax.dot_general(gr[:, own], enc_rows(i - 2), (((0,), (0,)), ((), ())), preferred_element_type=F32)
-        for c in range(NCH):
-            @pl.when(chunk(i - 2, c)[2])
-            def _():
-                gh_copy(i - 2, c, h_v, par).start()
 
     trips = (n_iter + 3) // 2
 
     @pl.loop(0, trips)
     def _(ii):
-        stage(2 * ii, z0_v, z1_v, g1_v, g0_v, h0_v, 0)
-        stage(2 * ii + 1, z1_v, z0_v, g0_v, g1_v, h1_v, 1)
-
-    gh_wait(2 * trips - 4, h0_v, 0)
-    gh_wait(2 * trips - 3, h1_v, 1)
+        i = 2 * ii
+        slot = lax.rem(ii, 2)
+        gh_wait(i - 6, h0_v.at[slot], 2 * slot)
+        gh_wait(i - 5, h1_v.at[slot], 2 * slot + 1)
+        stage(i, z0_v, z1_v, g1_v, g0_v, h0_v.at[slot])
+        stage(i + 1, z1_v, z0_v, g0_v, g1_v, h1_v.at[slot])
+        gh_start(i - 2, h0_v.at[slot], 2 * slot)
+        gh_start(i - 1, h1_v.at[slot], 2 * slot + 1)
+
+    for back in (2, 1):
+        slot = lax.rem(trips - back + 2, 2)
+        gh_wait(2 * (trips - back) - 2, h0_v.at[slot], 2 * slot)
+        gh_wait(2 * (trips - back) - 1, h1_v.at[slot], 2 * slot + 1)
     gw_ref[...] = gwt_v[...].T
     loss_ref[...] = lacc_v[...].T[0:1, :] - blank_sum - log_z
 
-    @pl.loop(0, n_seq)
-    def _(b):
-        cnt = (in_len[b] + CH - 1) // CH
-        for j in range(n_per):
-            @pl.when(j >= cnt)
-            def _():
-                zero_copy(b, j).wait()
+    @pl.loop(0, n_seq * n_per - n_live)
+    def _(_):
+        zero_copy(0, 0).wait()
 
 
 def solution(mesh):
@@ -365,11 +428,11 @@
         smem = pl.BlockSpec(memory_space=pltpu.SMEM)
         anyspace = pl.BlockSpec(memory_space=pl.ANY)
         w_all = pl.pallas_call(
-            functools.partial(gather_kernel, n_dev),
+            gather_kernel,
             out_shape=jax.ShapeDtypeStruct((n_dev, hidden, n_cols), BF16),
             in_specs=[vmem],
             out_specs=vmem,
-            scratch_shapes=[pltpu.SemaphoreType.DMA((n_dev,)), pltpu.SemaphoreType.DMA((n_dev,))],
+            scratch_shapes=[pltpu.SemaphoreType.DMA((9,)), pltpu.SemaphoreType.DMA((9,))],
             compiler_params=pltpu.CompilerParams(collective_id=0, has_side_effects=True),
             name="gather_w",
         )(w_loc)
@@ -389,6 +452,8 @@
                 pltpu.VMEM((hidden, n_vocab), BF16),
                 pltpu.VMEM((n_vocab, hidden), BF16),
                 pltpu.VMEM((192, n_vocab), BF16),
+                pltpu.VMEM((192, n_vocab), BF16),
+                pltpu.VMEM((512, hidden), BF16),
                 pltpu.VMEM((512, hidden), BF16),
                 pltpu.VMEM((n_seq * PITCH, 128), F32),
                 pltpu.VMEM((n_frames * 48, 128), F32),
@@ -399,8 +464,8 @@
                 pltpu.VMEM((NCH * CH, n_vocab), F32),
                 pltpu.VMEM((NCH * CH, n_vocab), BF16),
                 pltpu.VMEM((NCH * CH, n_vocab), BF16),
-                pltpu.VMEM((NCH * CH, hidden), F32),
-                pltpu.VMEM((NCH * CH, hidden), F32),
+                pltpu.VMEM((2, NCH * CH, hidden), F32),
+                pltpu.VMEM((2, NCH * CH, hidden), F32),
                 pltpu.VMEM((NCH * CH, 128), F32),
                 pltpu.VMEM((NCH * CH, 128), F32),
                 pltpu.VMEM((NCH * CH, 128), F32),
@@ -408,12 +473,12 @@
                 pltpu.VMEM((n_seq, 128), F32),
                 pltpu.VMEM((CH, hidden), F32),
                 pltpu.VMEM((8, 128), jnp.int32),
-                pltpu.SMEM((n_seq * n_per + 10 * NCH,), jnp.int32),
-                pltpu.SMEM((n_seq * n_per + 10 * NCH,), jnp.int32),
+                pltpu.SMEM((n_seq * n_per + 3 * PAD,), jnp.int32),
+                pltpu.SMEM((n_seq * n_per + 3 * PAD,), jnp.int32),
                 pltpu.SMEM((8, 128), jnp.int32),
                 pltpu.SemaphoreType.DMA((n_grp,)),
                 pltpu.SemaphoreType.DMA((n_dev,)),
-                pltpu.SemaphoreType.DMA((2, NCH)),
+                pltpu.SemaphoreType.DMA((4, NCH)),
                 pltpu.SemaphoreType.DMA,
                 pltpu.SemaphoreType.DMA,
             ],

time: 151 us -> 134 us (0.89)
  Pallas kernels: 149 us -> 133 us
    pallas_call x1, Pallas kernels: 131 us -> 119 us  [device_fn(): pl.pallas_call(functools.partial(ctc_kernel, n_seq, n_frames, n_lab), out...]
    pallas_call x1, Pallas kernels: 18.1 us -> 13.8 us  [device_fn(): pl.pallas_call(gather_kernel, out_shape=jax.ShapeDtypeStruct((n_dev, hidd...]
where the time goes in v1:
time: 134 us; the launch traced here: 133 us
  Pallas kernels  133 us (99%)
    pallas_call x1, Pallas kernels, device_fn(): pl.pallas_call(functools.partial(ctc_kernel, n_seq, n_frames, n_lab), out...  119 us
    pallas_call x1, Pallas kernels, device_fn(): pl.pallas_call(gather_kernel, out_shape=jax.ShapeDtypeStruct((n_dev, hidd...  13.8 us

profile of v1, /device:TPU:1, one launch (start us, length us, event | category | flops | bytes accessed | tf_op | source)
XLA Modules:
  0.0 133.5 jit_solution(2847012142270014072)
XLA Ops:
  0.6 13.8 %gather_w.1.wg_hbm = bf16[8,512,128]{2,1,0:T(8,128)(2,1)} custom-call(bf16[512,128]{1,0:T(8,128)(2,1)} %w_ref.1), custom_call_target="tpu_custom_call" | custom-call | tf_op jit(solution)/shard_map/gather_w/pallas_call | solution.py:430
  14.5 119.0 %ctc.1 = (f32[1,128]{1,0:T(1,128)}, f32[512,128]{1,0:T(8,128)}, f32[24576,512]{1,0:T(8,128)}) custom-call(s32[128]{0:T(128)} %in_len.1, s32[48,128]{1,0:T(8,128)} %bitcast.7, s32[1,128]{1,0:T(1,128)} %bitcast.8, s32[1,128]{1,0:T(1,128)} %bitcast.9, bf16[24576,512]{1,0:T(8,128)(2,1)} %bitcast.6, bf16[8,512,128]{2,1,0:T(8,128)(2,1)} %gather_w.1.wg_hbm), custom_call_target="tpu_custom_call" | custom-call | tf_op jit(solution)/shard_map/ctc/pallas_call | solution.py:441

commit v2 on v1

--- a/solution.py
+++ b/solution.py
@@ -9,9 +9,9 @@
 
 NEG_FILL = -1.0e30
 CH = 32
-NCH = 8
-PAD = 8 * NCH
-PITCH = 104
+NCH = 16
+PAD = 6 * NCH
+PITCH = 136
 DUMMY = 55
 UNR = 4
 AHEAD = 6
@@ -74,7 +74,7 @@
     n_seq, n_frames, n_lab,
     in_len, labt_ref, inrow_ref, lenrow_ref, enc_hbm, wg_hbm,
     loss_ref, gw_ref, ghs_hbm,
-    enc_v, w_v, wt_v, oh0_v, oh1_v, gl0_v, gl1_v, eo_v, et_v, ab_v, inv_v, nxt_v, z0_v, z1_v, g0_v, g1_v, h0_v, h1_v, top_v, sum_v, lse_v, gwt_v, lacc_v, zero_v, flag_v,
+    enc_v, w_v, wt_v, oh0_v, oh1_v, gl0_v, gl1_v, eo_v, et_v, ab_v, inv_v, nxt_v, z0_v, z1_v, g0_v, g1_v, h0_v, h1_v, top0_v, top1_v, sum0_v, sum1_v, lse0_v, lse1_v, gwt_v, lacc_v, zero_v, flag_v,
     tabb, tabt, flag_s, enc_sem, w_sem, gh_sem, zero_sem, flag_sem,
 ):
     me = lax.axis_index("tp")
@@ -96,15 +96,8 @@
     for g in range(AHEAD):
         enc_copy(g).start()
 
-    for ref in (zero_v, lacc_v, gwt_v, z0_v, z1_v, g0_v, g1_v):
+    for ref in (zero_v, lacc_v, gwt_v, z1_v, lse1_v, g0_v, g1_v):
         ref[...] = jnp.zeros_like(ref)
-    for j in range(PAD):
-        tabb[j] = 0
-        tabt[j] = 0
-
-    def zero_copy(b, j):
-        return pltpu.make_async_copy(zero_v, ghs_hbm.at[pl.ds(pl.multiple_of(b * n_frames + j * CH, CH), CH)], zero_sem)
-
     sub48 = lax.broadcasted_iota(jnp.int32, (48, 128), 0)
     in_row = inrow_ref[...]
     len_row = lenrow_ref[...]
@@ -139,15 +132,13 @@
 
     def list_group(g, n):
         for k in range(4):
-            b = jnp.minimum(4 * g + k, n_seq - 1)
-            cnt = jnp.where(g < n_grp, (in_len[b] + CH - 1) // CH, n_per)
+            b = 4 * g + k
+            cnt = (in_len[jnp.minimum(b, n_seq - 1)] + CH - 1) // CH
+            dead = n_seq * n_per - 1 - (b * n_per - n)
             for j in range(n_per):
-                tabb[PAD + n + j] = b
-                tabt[PAD + n + j] = j * CH
-
-                @pl.when(j >= cnt)
-                def _():
-                    zero_copy(b, j).start()
+                slot = jnp.where(g < n_grp, PAD + jnp.where(j < cnt, n + j, dead - (j - cnt)), j)
+                tabb[slot] = b
+                tabt[slot] = j * CH
             n = n + jnp.where(g < n_grp, cnt, 0)
         return n
 
@@ -174,7 +165,7 @@
             b = 4 * g + k
             x = enc_v[pl.ds(pl.multiple_of(b * n_frames, n_frames), n_frames), :]
             e = lax.dot_general(x, gl_v[k * 128:(k + 1) * 128, :], (((1,), (1,)), ((), ())), preferred_element_type=F32)
-            eo_v[pl.ds(pl.multiple_of(b * PITCH, 8), mid), :] = jnp.where(lane_mid < 64, e[0:mid], e[mid:n_frames])
+            eo_v[pl.ds(b, mid, stride=PITCH), :] = jnp.where(lane_mid < 64, e[0:mid], e[mid:n_frames])
 
     build_hot(0, oh0_v)
 
@@ -199,14 +190,23 @@
 
     n_live = lax.fori_loop(0, n_grp // 2 + 1, emit_pair, 0)
     for j in range(PAD):
-        tabb[PAD + n_live + j] = 0
-        tabt[PAD + n_live + j] = 0
+        for base in (0, PAD + n_seq * n_per):
+            tabb[base + j] = 0
+            tabt[base + j] = 0
     n_iter = (n_live + NCH - 1) // NCH
+
+    def zero_copy(k):
+        row = pl.multiple_of(tabb[PAD + k] * n_frames + tabt[PAD + k], CH)
+        return pltpu.make_async_copy(zero_v, ghs_hbm.at[pl.ds(row, CH)], zero_sem)
+
+    @pl.loop(n_iter * NCH, n_seq * n_per)
+    def _(k):
+        zero_copy(k).start()
 
     def turn_emissions(jj, acc):
         for u in range(UNR):
             j = jj * UNR + u
-            turned = eo_v[pl.ds(j, n_seq, stride=PITCH), :].T
+            turned = eo_v[pl.ds(pl.multiple_of(j * PITCH, 8), n_seq), :].T
             low = turned[48:49]
             high = turned[112:113]
             et_v[pl.ds(pl.multiple_of(j * 48, 8), 48), :] = turned[0:48] - low
@@ -218,7 +218,6 @@
 
     neg8 = jnp.full((8, 128), NEG_FILL, F32)
     sub56 = lax.broadcasted_iota(jnp.int32, (56, 128), 0)
-    skip56 = jnp.concatenate([jnp.where(skip, 1.0, 0.0), jnp.zeros((8, 128), F32)], axis=0) > 0.5
 
     def emit_at(t):
         return et_v[pl.ds(pl.multiple_of(t * 48, 8), 48), :]
@@ -234,7 +233,7 @@
     def beta_step(t, blk, lab):
         emitted = lab + emit_at(t + 1)
         blk_new = lse2(blk, jnp.concatenate([emitted, neg8], axis=0))
-        via = jnp.where(skip56, blk_new, blk)
+        via = jnp.concatenate([jnp.where(skip, blk_new[0:48], blk[0:48]), blk_new[48:56]], axis=0)
         lab_new = lse2(emitted, pltpu.roll(via, 55, 0)[0:48])
         live = t + 1 < in_row
         return jnp.where(live, blk_new, blk), jnp.where(live, lab_new, lab)
@@ -302,14 +301,14 @@
             low = ab_v[pl.ds(pl.multiple_of(j * 104, 8), 56), :]
             high = ab_v[pl.ds(pl.multiple_of((j + mid) * 104, 8), 56), :]
             turned = jnp.concatenate([low, zero8, high, zero8], axis=0).T
-            eo_v[pl.ds(j, n_seq, stride=PITCH), :] = turned + take_lanes(turned, nxt_v[...])
+            eo_v[pl.ds(pl.multiple_of(j * PITCH, 8), n_seq), :] = turned + take_lanes(turned, nxt_v[...])
 
     flag_copy.wait()
 
     def more_rounds(b):
         @pl.when(flag_s[0, b] > 1)
         def _():
-            rows = pl.ds(pl.multiple_of(b * PITCH, 8), mid)
+            rows = pl.ds(b, mid, stride=PITCH)
             count = flag_s[0, b]
             rounds = sum((count >= 2 ** r).astype(jnp.int32) for r in range(1, 6))
 
@@ -336,7 +335,7 @@
 
     def chunk(i, c):
         idx = i * NCH + c
-        return tabb[idx + PAD], tabt[idx + PAD], (idx >= 0) & (idx < n_live)
+        return tabb[idx + PAD], tabt[idx + PAD], (i >= 0) & (i < n_iter)
 
     def enc_rows(i):
         parts = []
@@ -345,51 +344,47 @@
             parts.append(enc_v[pl.ds(pl.multiple_of(b * n_frames + t0, CH), CH), :])
         return jnp.concatenate(parts, axis=0)
 
-    def gh_copy(i, c, h_v, par):
-        b, t0, _ = chunk(i, c)
-        row = pl.multiple_of(b * n_frames + t0, CH)
-        return pltpu.make_async_copy(h_v.at[pl.ds(c * CH, CH)], ghs_hbm.at[pl.ds(row, CH)], gh_sem.at[par, c])
-
     def gh_wait(i, h_v, par):
+        @pl.when((i >= 0) & (i < n_iter))
+        def _():
+            pltpu.make_async_copy(h_v, ghs_hbm.at[pl.ds(0, NCH * CH)], gh_sem.at[par]).wait()
+
+    def gh_start(i, h_v, par):
+        @pl.when((i >= 0) & (i < n_iter))
+        def _():
+            for c in range(NCH):
+                b, t0, _ = chunk(i, c)
+                row = pl.multiple_of(b * n_frames + t0, CH)
+                pltpu.make_async_copy(h_v.at[pl.ds(c * CH, CH)], ghs_hbm.at[pl.ds(row, CH)], gh_sem.at[par]).start()
+
+    def stage(i, zw, zr, lse_w, lse_r, top_v, sum_v, gwr, gr, h_v):
+        zw[...] = jnp.dot(enc_rows(i), w_v[...], preferred_element_type=F32)
+        h_v[...] = jnp.dot(gr[...], wt_v[...], preferred_element_type=F32)
+        gwt_v[...] += lax.dot_general(gr[:, own], enc_rows(i - 2), (((0,), (0,)), ((), ())), preferred_element_type=F32)
         for c in range(NCH):
-            @pl.when(chunk(i, c)[2])
-            def _():
-                gh_copy(i, c, h_v, par).wait()
-
-    def gh_start(i, h_v, par):
-        for c in range(NCH):
-            @pl.when(chunk(i, c)[2])
-            def _():
-                gh_copy(i, c, h_v, par).start()
-
-    def stage(i, zw, zr, gwr, gr, h_v):
-        zw[...] = jnp.dot(enc_rows(i), w_v[...], preferred_element_type=F32)
+            b, t0, ok = chunk(i - 1, c)
+            rows = slice(c * CH, (c + 1) * CH)
+            live = row_ids < jnp.where(ok, in_len[b], 0) - t0
+            lse = lse_r[rows, :]
+            lacc_v[pl.ds(b, 1), :] += jnp.sum(jnp.where(live, lse, 0.0), axis=0, keepdims=True)
+            lse = jnp.where(live, lse, 3.0e38)
+            upper = (t0 >= mid).astype(jnp.int32)
+            occ = jnp.where(live, eo_v[pl.ds(b + (t0 - upper * mid) * PITCH, CH, stride=PITCH), :], 0.0)
+            inv = inv_v[pl.ds(pl.multiple_of(b * 8, 8), 8), :] + upper * 64
+            for j in range(n_blk):
+                cols = slice(j * 128, (j + 1) * 128)
+                col_occ = take_lanes(occ, jnp.broadcast_to(inv[j:j + 1], (CH, 128)))
+                gwr[rows, cols] = (jnp.exp(zr[rows, cols] - lse) - col_occ).astype(BF16)
         for r in range(NCH * CH // 8):
             rows = slice(r * 8, (r + 1) * 8)
-            z = zr[rows, :]
+            z = zw[rows, :]
             parts = [z[:, j * 128:(j + 1) * 128] for j in range(n_blk)]
             top = functools.reduce(jnp.maximum, parts)
             top_v[rows, :] = top
             sum_v[rows, :] = functools.reduce(jnp.add, [jnp.exp(part - top) for part in parts])
         tops = top_v[...]
         top = jnp.max(tops, axis=1, keepdims=True)
-        lse_v[...] = jnp.broadcast_to(top + jnp.log(jnp.sum(sum_v[...] * jnp.exp(tops - top), axis=1, keepdims=True)), (NCH * CH, 128))
-        for c in range(NCH):
-            b, t0, ok = chunk(i - 1, c)
-            rows = slice(c * CH, (c + 1) * CH)
-            live = row_ids < jnp.where(ok, in_len[b], 0) - t0
-            lse = lse_v[rows, :]
-            lacc_v[pl.ds(b, 1), :] += jnp.sum(jnp.where(live, lse, 0.0), axis=0, keepdims=True)
-            lse = jnp.where(live, lse, 3.0e38)
-            upper = (t0 >= mid).astype(jnp.int32)
-            occ = jnp.where(live, eo_v[pl.ds(pl.multiple_of(b * PITCH + t0 - upper * mid, 8), CH), :], 0.0)
-            inv = inv_v[pl.ds(pl.multiple_of(b * 8, 8), 8), :] + upper * 64
-            for j in range(n_blk):
-                cols = slice(j * 128, (j + 1) * 128)
-                col_occ = take_lanes(occ, jnp.broadcast_to(inv[j:j + 1], (CH, 128)))
-                gwr[rows, cols] = (jnp.exp(zr[rows, cols] - lse) - col_occ).astype(BF16)
-        h_v[...] = jnp.dot(gr[...], wt_v[...], preferred_element_type=F32)
-        gwt_v[...] += lax.dot_general(gr[:, own], enc_rows(i - 2), (((0,), (0,)), ((), ())), preferred_element_type=F32)
+        lse_w[...] = jnp.broadcast_to(top + jnp.log(jnp.sum(sum_v[...] * jnp.exp(tops - top), axis=1, keepdims=True)), (NCH * CH, 128))
 
     trips = (n_iter + 3) // 2
 
@@ -399,8 +394,8 @@
         slot = lax.rem(ii, 2)
         gh_wait(i - 6, h0_v.at[slot], 2 * slot)
         gh_wait(i - 5, h1_v.at[slot], 2 * slot + 1)
-        stage(i, z0_v, z1_v, g1_v, g0_v, h0_v.at[slot])
-        stage(i + 1, z1_v, z0_v, g0_v, g1_v, h1_v.at[slot])
+        stage(i, z0_v, z1_v, lse0_v, lse1_v, top0_v, sum0_v, g1_v, g0_v, h0_v.at[slot])
+        stage(i + 1, z1_v, z0_v, lse1_v, lse0_v, top1_v, sum1_v, g0_v, g1_v, h1_v.at[slot])
         gh_start(i - 2, h0_v.at[slot], 2 * slot)
         gh_start(i - 1, h1_v.at[slot], 2 * slot + 1)
 
@@ -411,9 +406,9 @@
     gw_ref[...] = gwt_v[...].T
     loss_ref[...] = lacc_v[...].T[0:1, :] - blank_sum - log_z
 
-    @pl.loop(0, n_seq * n_per - n_live)
-    def _(_):
-        zero_copy(0, 0).wait()
+    @pl.loop(n_iter * NCH, n_seq * n_per)
+    def _(k):
+        zero_copy(k).wait()
 
 
 def solution(mesh):
@@ -455,7 +450,7 @@
                 pltpu.VMEM((192, n_vocab), BF16),
                 pltpu.VMEM((512, hidden), BF16),
                 pltpu.VMEM((512, hidden), BF16),
-                pltpu.VMEM((n_seq * PITCH, 128), F32),
+                pltpu.VMEM((n_frames // 2 * PITCH, 128), F32),
                 pltpu.VMEM((n_frames * 48, 128), F32),
                 pltpu.VMEM((n_frames * 104, 128), F32),
                 pltpu.VMEM((n_seq * n_dev, 128), jnp.int32),
@@ -469,6 +464,9 @@
                 pltpu.VMEM((NCH * CH, 128), F32),
                 pltpu.VMEM((NCH * CH, 128), F32),
                 pltpu.VMEM((NCH * CH, 128), F32),
+                pltpu.VMEM((NCH * CH, 128), F32),
+                pltpu.VMEM((NCH * CH, 128), F32),
+                pltpu.VMEM((NCH * CH, 128), F32),
                 pltpu.VMEM((n_cols, hidden), F32),
                 pltpu.VMEM((n_seq, 128), F32),
                 pltpu.VMEM((CH, hidden), F32),
@@ -478,7 +476,7 @@
                 pltpu.SMEM((8, 128), jnp.int32),
                 pltpu.SemaphoreType.DMA((n_grp,)),
                 pltpu.SemaphoreType.DMA((n_dev,)),
-                pltpu.SemaphoreType.DMA((4, NCH)),
+                pltpu.SemaphoreType.DMA((4,)),
                 pltpu.SemaphoreType.DMA,
                 pltpu.SemaphoreType.DMA,
             ],

time: 134 us -> 125 us (0.933)
  Pallas kernels: 133 us -> 123 us
    pallas_call x1, Pallas kernels: 119 us -> 109 us  [device_fn(): pl.pallas_call(functools.partial(ctc_kernel, n_seq, n_frames, n_lab), out...]
where the time goes in v2:
time: 125 us; the launch traced here: 124 us
  Pallas kernels  123 us (98%)
    pallas_call x1, Pallas kernels, device_fn(): pl.pallas_call(functools.partial(ctc_kernel, n_seq, n_frames, n_lab), out...  109 us
    pallas_call x1, Pallas kernels, device_fn(): pl.pallas_call(gather_kernel, out_shape=jax.ShapeDtypeStruct((n_dev, hidd...  13.8 us

profile of v2, /device:TPU:1, one launch (start us, length us, event | category | flops | bytes accessed | tf_op | source)
XLA Modules:
  0.0 123.8 jit_solution(14902473549665802151)
XLA Ops:
  0.6 13.8 %gather_w.1.wg_hbm = bf16[8,512,128]{2,1,0:T(8,128)(2,1)} custom-call(bf16[512,128]{1,0:T(8,128)(2,1)} %w_ref.1), custom_call_target="tpu_custom_call" | custom-call | tf_op jit(solution)/shard_map/gather_w/pallas_call | solution.py:425
  14.5 109.4 %ctc.1 = (f32[1,128]{1,0:T(1,128)}, f32[512,128]{1,0:T(8,128)}, f32[24576,512]{1,0:T(8,128)}) custom-call(s32[128]{0:T(128)} %in_len.1, s32[48,128]{1,0:T(8,128)} %bitcast.7, s32[1,128]{1,0:T(1,128)} %bitcast.8, s32[1,128]{1,0:T(1,128)} %bitcast.9, bf16[24576,512]{1,0:T(8,128)(2,1)} %bitcast.6, bf16[8,512,128]{2,1,0:T(8,128)(2,1)} %gather_w.1.wg_hbm), custom_call_target="tpu_custom_call" | custom-call | tf_op jit(solution)/shard_map/ctc/pallas_call | solution.py:436

commit v3 on v2

--- a/solution.py
+++ b/solution.py
@@ -13,7 +13,6 @@
 PAD = 6 * NCH
 PITCH = 136
 DUMMY = 55
-UNR = 4
 AHEAD = 6
 MESH = pl.DeviceIdType.MESH
 F32 = jnp.float32
@@ -75,7 +74,7 @@
     in_len, labt_ref, inrow_ref, lenrow_ref, enc_hbm, wg_hbm,
     loss_ref, gw_ref, ghs_hbm,
     enc_v, w_v, wt_v, oh0_v, oh1_v, gl0_v, gl1_v, eo_v, et_v, ab_v, inv_v, nxt_v, z0_v, z1_v, g0_v, g1_v, h0_v, h1_v, top0_v, top1_v, sum0_v, sum1_v, lse0_v, lse1_v, gwt_v, lacc_v, zero_v, flag_v,
-    tabb, tabt, flag_s, enc_sem, w_sem, gh_sem, zero_sem, flag_sem,
+    tabb, tabt, rep_s, flag_s, enc_sem, w_sem, gh_sem, zero_sem, flag_sem,
 ):
     me = lax.axis_index("tp")
     n_vocab = w_v.shape[1]
@@ -111,7 +110,8 @@
         nxt = jnp.where(same, sub48 + d, nxt)
         later = later + jnp.where(same, 1, 0)
     nxt_f = jnp.concatenate([nxt.astype(F32), jnp.full((16, 128), float(DUMMY), F32)], axis=0)
-    nxt_v[...] = jnp.concatenate([nxt_f, nxt_f + 64.0], axis=0).T.astype(jnp.int32)
+    nxt_v[0:n_seq] = jnp.concatenate([nxt_f, nxt_f + 64.0], axis=0).T.astype(jnp.int32)
+    nxt_v[n_seq:n_seq + 8] = jnp.full((8, 128), DUMMY, jnp.int32)
     flag_v[...] = jnp.broadcast_to(jnp.max(later.astype(F32), axis=0, keepdims=True), (8, 128)).astype(jnp.int32)
     flag_copy = pltpu.make_async_copy(flag_v, flag_s, flag_sem)
     flag_copy.start()
@@ -203,18 +203,17 @@
     def _(k):
         zero_copy(k).start()
 
-    def turn_emissions(jj, acc):
-        for u in range(UNR):
-            j = jj * UNR + u
-            turned = eo_v[pl.ds(pl.multiple_of(j * PITCH, 8), n_seq), :].T
-            low = turned[48:49]
-            high = turned[112:113]
-            et_v[pl.ds(pl.multiple_of(j * 48, 8), 48), :] = turned[0:48] - low
-            et_v[pl.ds(pl.multiple_of((j + mid) * 48, 8), 48), :] = turned[64:112] - high
-            acc = acc + jnp.where(j < in_row, low, 0.0) + jnp.where(j + mid < in_row, high, 0.0)
-        return acc
-
-    blank_sum = lax.fori_loop(0, mid // UNR, turn_emissions, jnp.zeros((1, 128), F32))
+    def turn_in(j, acc):
+        turned = eo_v[pl.ds(pl.multiple_of(j * PITCH, 8), n_seq), :].T
+        low = turned[48:49]
+        high = turned[112:113]
+        et_v[pl.ds(pl.multiple_of(j * 48, 8), 48), :] = turned[0:48] - low
+        et_v[pl.ds(pl.multiple_of((j + mid) * 48, 8), 48), :] = turned[64:112] - high
+        return acc + jnp.where(j < in_row, low, 0.0) + jnp.where(j + mid < in_row, high, 0.0)
+
+    blank_sum = jnp.zeros((1, 128), F32)
+    for j in (0, 1, mid - 1):
+        blank_sum = turn_in(j, blank_sum)
 
     neg8 = jnp.full((8, 128), NEG_FILL, F32)
     sub56 = lax.broadcasted_iota(jnp.int32, (56, 128), 0)
@@ -261,7 +260,27 @@
         keep(t, b_blk, b_lab)
         return a_blk, a_lab, b_blk, b_lab
 
-    a_blk, a_lab, b_blk, b_lab = lax.fori_loop(1, mid, first_half, (a_blk, a_lab, b_blk, b_lab))
+    def first_quarter(k, state):
+        new = first_half(k, state[:4])
+        return (*new, turn_in(mid - 1 - k, turn_in(k + 1, state[4])))
+
+    quarter = mid // 2
+    a_blk, a_lab, b_blk, b_lab, blank_sum = lax.fori_loop(1, quarter - 1, first_quarter, (a_blk, a_lab, b_blk, b_lab, blank_sum))
+    blank_sum = turn_in(quarter, blank_sum)
+
+    flag_copy.wait()
+
+    def second_quarter(k, state):
+        n = state[4]
+        for u in range(3):
+            b = jnp.minimum(3 * (k - quarter + 1) + u, n_seq)
+            rep_s[n] = b
+            n = n + jnp.where((b < n_seq) & (flag_s[0, jnp.minimum(b, n_seq - 1)] > 0), 1, 0)
+        return (*first_half(k, state[:4]), n)
+
+    a_blk, a_lab, b_blk, b_lab, n_rep = lax.fori_loop(quarter - 1, mid, second_quarter, (a_blk, a_lab, b_blk, b_lab, 0))
+    for u in range(4):
+        rep_s[n_rep + u] = n_seq
 
     m_blk, m_lab = beta_step(mid - 1, b_blk, b_lab)
     s_blk = a_blk + m_blk
@@ -277,6 +296,14 @@
         occ_lab = jnp.exp(ab_v[pl.ds(row + 56, 48), :] + (lab - log_z))
         ab_v[pl.ds(row, 48), :] = occ_lab
         ab_v[pl.ds(row + 48, 8), :] = jnp.where(sub8 == 0, occ_blk, 0.0)
+
+    zero8 = jnp.zeros((8, 128), F32)
+
+    def turn_out(j):
+        low = ab_v[pl.ds(pl.multiple_of(j * 104, 8), 56), :]
+        high = ab_v[pl.ds(pl.multiple_of((j + mid) * 104, 8), 56), :]
+        turned = jnp.concatenate([low, zero8, high, zero8], axis=0).T
+        eo_v[pl.ds(pl.multiple_of(j * PITCH, 8), n_seq), :] = turned
 
     def second_half(k, state):
         a_blk, a_lab, b_blk, b_lab = state
@@ -287,29 +314,35 @@
         b_blk, b_lab = beta_step(t, b_blk, b_lab)
         return a_blk, a_lab, b_blk, b_lab
 
+    def last_quarter(k, state):
+        turn_out(k - 2 - mid)
+        turn_out(n_frames + 1 - k)
+        return second_half(k, state)
+
     a_blk, a_lab = alpha_step(mid, a_blk, a_lab)
-    a_blk, a_lab, b_blk, b_lab = lax.fori_loop(mid + 1, n_frames, second_half, (a_blk, a_lab, m_blk, m_lab))
+    state = lax.fori_loop(mid + 1, mid + quarter + 2, second_half, (a_blk, a_lab, m_blk, m_lab))
+    a_blk, a_lab, b_blk, b_lab = lax.fori_loop(mid + quarter + 2, n_frames, last_quarter, state)
     put_occ(n_frames - 1, a_blk, a_lab)
     put_occ(0, b_blk, b_lab)
-
-    zero8 = jnp.zeros((8, 128), F32)
-
-    @pl.loop(0, mid // UNR)
-    def _(jj):
-        for u in range(UNR):
-            j = jj * UNR + u
-            low = ab_v[pl.ds(pl.multiple_of(j * 104, 8), 56), :]
-            high = ab_v[pl.ds(pl.multiple_of((j + mid) * 104, 8), 56), :]
-            turned = jnp.concatenate([low, zero8, high, zero8], axis=0).T
-            eo_v[pl.ds(pl.multiple_of(j * PITCH, 8), n_seq), :] = turned + take_lanes(turned, nxt_v[...])
-
-    flag_copy.wait()
-
-    def more_rounds(b):
-        @pl.when(flag_s[0, b] > 1)
+    for j in (mid - 2, 1, mid - 1, 0):
+        turn_out(j)
+
+    @pl.loop(0, (n_rep + 3) // 4)
+    def _(q):
+        seqs = [rep_s[4 * q + u] for u in range(4)]
+        occs = [eo_v[pl.ds(b, mid, stride=PITCH), :] for b in seqs]
+        links = [nxt_v[pl.ds(b, 1), :] for b in seqs]
+        for b, occ, link in zip(seqs, occs, links):
+            eo_v[pl.ds(b, mid, stride=PITCH), :] = occ + take_lanes(occ, jnp.broadcast_to(link, (mid, 128)))
+
+    @pl.loop(0, n_rep)
+    def _(r):
+        b = rep_s[r]
+        count = flag_s[0, b]
+
+        @pl.when(count > 1)
         def _():
             rows = pl.ds(b, mid, stride=PITCH)
-            count = flag_s[0, b]
             rounds = sum((count >= 2 ** r).astype(jnp.int32) for r in range(1, 6))
 
             def more(_, link):
@@ -319,16 +352,6 @@
                 return link
 
             lax.fori_loop(0, rounds, more, jnp.broadcast_to(nxt_v[pl.ds(b, 1), :], (8, 128)))
-
-    @pl.loop(0, n_seq // 16)
-    def _(bb):
-        most = functools.reduce(jnp.maximum, [flag_s[0, bb * 16 + u] for u in range(16)])
-
-        @pl.when(most > 1)
-        def _():
-            @pl.loop(0, 16)
-            def _(u):
-                more_rounds(bb * 16 + u)
 
     row_ids = lax.broadcasted_iota(jnp.int32, (CH, 128), 0)
     own = pl.ds(pl.multiple_of(me * 128, 128), 128)
@@ -454,7 +477,7 @@
                 pltpu.VMEM((n_frames * 48, 128), F32),
                 pltpu.VMEM((n_frames * 104, 128), F32),
                 pltpu.VMEM((n_seq * n_dev, 128), jnp.int32),
-                pltpu.VMEM((n_seq, 128), jnp.int32),
+                pltpu.VMEM((n_seq + 8, 128), jnp.int32),
                 pltpu.VMEM((NCH * CH, n_vocab), F32),
                 pltpu.VMEM((NCH * CH, n_vocab), F32),
                 pltpu.VMEM((NCH * CH, n_vocab), BF16),
@@ -473,6 +496,7 @@
                 pltpu.VMEM((8, 128), jnp.int32),
                 pltpu.SMEM((n_seq * n_per + 3 * PAD,), jnp.int32),
                 pltpu.SMEM((n_seq * n_per + 3 * PAD,), jnp.int32),
+                pltpu.SMEM((n_seq + 8,), jnp.int32),
                 pltpu.SMEM((8, 128), jnp.int32),
                 pltpu.SemaphoreType.DMA((n_grp,)),
                 pltpu.SemaphoreType.DMA((n_dev,)),

time: 125 us -> 119 us (0.952)
  Pallas kernels: 123 us -> 118 us
    pallas_call x1, Pallas kernels: 109 us -> 104 us  [device_fn(): pl.pallas_call(functools.partial(ctc_kernel, n_seq, n_frames, n_lab), out...]
where the time goes in v3:
time: 119 us
  Pallas kernels  118 us (99%)
    pallas_call x1, Pallas kernels, device_fn(): pl.pallas_call(functools.partial(ctc_kernel, n_seq, n_frames, n_lab), out...  104 us
    pallas_call x1, Pallas kernels, device_fn(): pl.pallas_call(gather_kernel, out_shape=jax.ShapeDtypeStruct((n_dev, hidd...  13.8 us

profile of v3, /device:TPU:1, one launch (start us, length us, event | category | flops | bytes accessed | tf_op | source)
XLA Modules:
  0.0 118.6 jit_solution(16332823329949799208)
XLA Ops:
  0.6 13.8 %gather_w.1.wg_hbm = bf16[8,512,128]{2,1,0:T(8,128)(2,1)} custom-call(bf16[512,128]{1,0:T(8,128)(2,1)} %w_ref.1), custom_call_target="tpu_custom_call" | custom-call | tf_op jit(solution)/shard_map/gather_w/pallas_call | solution.py:448
  14.5 104.2 %ctc.1 = (f32[1,128]{1,0:T(1,128)}, f32[512,128]{1,0:T(8,128)}, f32[24576,512]{1,0:T(8,128)}) custom-call(s32[128]{0:T(128)} %in_len.1, s32[48,128]{1,0:T(8,128)} %bitcast.7, s32[1,128]{1,0:T(1,128)} %bitcast.8, s32[1,128]{1,0:T(1,128)} %bitcast.9, bf16[24576,512]{1,0:T(8,128)(2,1)} %bitcast.6, bf16[8,512,128]{2,1,0:T(8,128)(2,1)} %gather_w.1.wg_hbm), custom_call_target="tpu_custom_call" | custom-call | tf_op jit(solution)/shard_map/ctc/pallas_call | solution.py:459
